TPU v7x, 32 devices: a whole 2x2x4 slice. The times are simulated.
32 devices in a mesh: row: 4 (over y, x), col: 8 (over z, core).
Axes of the slice: x: 2, y: 2, z: 4, core: 2. Of those that a mesh axis runs over, the one named last changes fastest.
Arguments:
- pair: bfloat16 [128, 128, 128], P('row', 'col'), may hold values from -6 to 6
- cotangent: bfloat16 [128, 128, 128], P('row', 'col'), may hold values from -6 to 6
- token_mask: int32 [128], replicated, may hold values 0 or 1
- out_in_proj: bfloat16 [128, 640], replicated, may hold values from -0.5 to 0.5
- out_out_proj: bfloat16 [128, 128], replicated, may hold values from -0.5 to 0.5
- in_in_proj: bfloat16 [128, 640], replicated, may hold values from -0.5 to 0.5
- in_out_proj: bfloat16 [128, 128], replicated, may hold values from -0.5 to 0.5
Outputs:
- updated_pair: bfloat16 [128, 128, 128], P('row', 'col')
- pair_grad: bfloat16 [128, 128, 128], P('row', 'col')
- out_in_grad: float32 [128, 640], replicated
- out_out_grad: float32 [128, 128], replicated
- in_in_grad: float32 [128, 640], replicated
- in_out_grad: float32 [128, 128], replicated
All inputs are finite; a program needn't handle non-finite values.
Results may differ from a plain program's by a relative error of at most 0.012.
Values may be sent and summed in bfloat16 or wider, within the bound.
No kernel may reach another device: no remote copies, remote signals or barrier semaphores. Data moves between devices by JAX's collectives and lax.ppermute only.
A program may use at most 128 MiB of HBM per device.

v0:
```python
import jax
import jax.numpy as jnp
from jax import lax
from jax.sharding import PartitionSpec as P

H = 128
EPSILON = 1e-05


def shortened(array):
    return jax.tree.map(lambda a: a.astype(jnp.bfloat16) if a.dtype == jnp.float32 else a, array)


def normalize(values):
    centre = jnp.mean(values, axis=-1, keepdims=True)
    shifted = values - centre
    spread = jnp.mean(shifted * shifted, axis=-1, keepdims=True)
    return shifted * lax.rsqrt(spread + EPSILON)


def gating(projected, pair_mask):
    left_value = projected[..., :H]
    left_gate = projected[..., H : 2 * H]
    right_value = projected[..., 2 * H : 3 * H]
    right_gate = projected[..., 3 * H : 4 * H]
    left_full = jax.nn.sigmoid(left_gate) * left_value * pair_mask
    right_full = jax.nn.sigmoid(right_gate) * right_value * pair_mask
    return (left_full, right_full, jax.nn.sigmoid(projected[..., 4 * H :]))


def cols_of(tiles):
    return jax.tree.map(
        lambda part, own: part.astype(own.dtype),
        lax.all_gather(shortened(tiles), "col", axis=1, tiled=True),
        tiles,
    )


def rows_of(tiles):
    return jax.tree.map(
        lambda part, own: part.astype(own.dtype),
        lax.all_gather(shortened(tiles), "row", axis=0, tiled=True),
        tiles,
    )


def to_row_blocks(panel):
    return lax.all_to_all(panel, "col", split_axis=0, concat_axis=1, tiled=True)


def to_col_blocks(panel):
    return lax.all_to_all(panel, "row", split_axis=1, concat_axis=0, tiled=True)


def outgoing_sum(left_tile, right_tile):
    row_panels = rows_of((left_tile, right_tile))
    left_panel = cols_of(left_tile)
    right_rows = to_row_blocks(row_panels[1])
    total = jnp.einsum("ikh,jkh->ijh", left_panel, right_rows, preferred_element_type=jnp.float32)
    return (total, row_panels)


def incoming_sum(left_tile, right_tile):
    col_panels = cols_of((left_tile, right_tile))
    right_all = rows_of(right_tile)
    left_cols = to_col_blocks(col_panels[0])
    total = jnp.einsum("kih,kjh->ijh", left_cols, right_all, preferred_element_type=jnp.float32)
    return (total, col_panels)


def outgoing_grads(tri_grad, row_panels):
    grad_cols = cols_of(tri_grad)
    grad_rows = to_col_blocks(grad_cols)
    left_grad = jnp.einsum(
        "ijh,jkh->ikh", grad_cols, row_panels[1], preferred_element_type=jnp.float32
    )
    right_grad = jnp.einsum(
        "ijh,ikh->jkh", grad_rows, row_panels[0], preferred_element_type=jnp.float32
    )
    return (left_grad, right_grad)


def incoming_grads(tri_grad, col_panels):
    grad_rows = rows_of(tri_grad)
    grad_cols = to_row_blocks(grad_rows)
    left_grad = jnp.einsum(
        "ijh,kjh->kih", grad_cols, col_panels[1], preferred_element_type=jnp.float32
    )
    right_grad = jnp.einsum(
        "kih,ijh->kjh", col_panels[0], grad_rows, preferred_element_type=jnp.float32
    )
    return (left_grad, right_grad)


def forward(pair_in, pair_mask, w_in, w_out, outgoing):
    pair_wide = pair_in.astype(jnp.float32)
    normed = normalize(pair_wide).astype(jnp.bfloat16)
    projected = jnp.dot(normed, w_in, preferred_element_type=jnp.float32)
    left_full, right_full, gate = gating(projected, pair_mask)
    left_tile = left_full.astype(jnp.bfloat16)
    right_tile = right_full.astype(jnp.bfloat16)
    if outgoing:
        triangle_sum, panels = outgoing_sum(left_tile, right_tile)
    else:
        triangle_sum, panels = incoming_sum(left_tile, right_tile)
    tri_normed = normalize(triangle_sum).astype(jnp.bfloat16)
    lifted = jnp.dot(tri_normed, w_out, preferred_element_type=jnp.float32)
    result = (pair_wide + gate * lifted).astype(jnp.bfloat16)
    saved = (pair_wide, normed, projected, gate, triangle_sum, tri_normed, lifted, panels)
    return (result, saved)


def backward(cotan, saved, pair_mask, w_in, w_out, outgoing):
    pair_wide, normed, projected, gate, triangle_sum, tri_normed, lifted, panels = saved
    cot_wide = cotan.astype(jnp.float32)
    lift_grad = gate * cot_wide
    gate_grad = lifted * cot_wide
    out_grad = jnp.einsum(
        "ijh,ijc->hc", tri_normed.astype(jnp.float32), lift_grad, precision=lax.Precision.HIGHEST
    )
    normed_tri_grad = jnp.dot(
        lift_grad, w_out.astype(jnp.float32).T, precision=lax.Precision.HIGHEST
    )
    tri_grad = jax.vjp(normalize, triangle_sum)[1](normed_tri_grad)[0].astype(jnp.bfloat16)
    if outgoing:
        left_grad, right_grad = outgoing_grads(tri_grad, panels)
    else:
        left_grad, right_grad = incoming_grads(tri_grad, panels)
    gate_vjp = jax.vjp(lambda values: gating(values, pair_mask), projected)[1]
    proj_grad = gate_vjp((left_grad, right_grad, gate_grad))[0]
    in_grad = jnp.einsum(
        "ijc,ijq->cq", normed.astype(jnp.float32), proj_grad, precision=lax.Precision.HIGHEST
    )
    normed_grad = jnp.dot(proj_grad, w_in.astype(jnp.float32).T, precision=lax.Precision.HIGHEST)
    pair_grad = (cot_wide + jax.vjp(normalize, pair_wide)[1](normed_grad)[0]).astype(jnp.bfloat16)
    return (pair_grad, in_grad, out_grad)


def local(pair, cotangent, token_mask, out_in_proj, out_out_proj, in_in_proj, in_out_proj):
    row_tile = pair.shape[0]
    col_tile = pair.shape[1]
    row_flags = lax.dynamic_slice_in_dim(
        token_mask, lax.axis_index("row") * row_tile, row_tile, 0
    ).astype(jnp.float32)
    col_flags = lax.dynamic_slice_in_dim(
        token_mask, lax.axis_index("col") * col_tile, col_tile, 0
    ).astype(jnp.float32)
    pair_mask = (row_flags[:, None] * col_flags[None, :])[:, :, None]
    middle, saved_out = forward(pair, pair_mask, out_in_proj, out_out_proj, True)
    updated, saved_in = forward(middle, pair_mask, in_in_proj, in_out_proj, False)
    middle_grad, in_in_part, in_out_part = backward(
        cotangent, saved_in, pair_mask, in_in_proj, in_out_proj, False
    )
    pair_grad, out_in_part, out_out_part = backward(
        middle_grad, saved_out, pair_mask, out_in_proj, out_out_proj, True
    )
    totals = lax.psum((out_in_part, out_out_part, in_in_part, in_out_part), ("row", "col"))
    tokens_all = row_tile * lax.axis_size("row")
    return (
        updated,
        pair_grad,
        totals[0] / tokens_all,
        totals[1] / tokens_all,
        totals[2] / tokens_all,
        totals[3] / tokens_all,
    )


def solution(mesh):
    return jax.shard_map(
        local,
        mesh=mesh,
        in_specs=(P("row", "col", None), P("row", "col", None), P(), P(), P(), P(), P()),
        out_specs=(P("row", "col", None), P("row", "col", None), P(), P(), P(), P()),
        check_vma=False,
    )
```

profile of v0, /device:TPU:0, one launch (start us, length us, event | category | flops | bytes accessed | tf_op | source)
XLA Modules:
  0.0 431.3 jit_solution(16462402712832531715)
XLA Ops:
  14.1 11.5 %all_gather.24 = bf16[128,16,128]{2,1,0:T(8,128)(2,1)S(1)} all-gather(bf16[32,16,128]{2,1,0:T(8,128)(2,1)S(1)} %get-tuple-element.33), channel_id=1, replica_groups=mesh['row'=4,'col'=8] {'row'}, dimensions={0}, use_global_device_ids=true | all-gather | bytes 655360 | tf_op jit(solution)/shard_map/all_gather | solution.py:42
  25.6 23.7 %all_to_all.72 = bf16[128,16,128]{2,1,0:T(8,128)(2,1)S(1)} all-to-all(bf16[128,16,128]{2,1,0:T(8,128)(2,1)S(1)} %all_gather.24), channel_id=1, replica_groups=mesh['row'=4,'col'=8] {'col'}, dimensions={0} | all-to-all | bytes 1048576 | tf_op jit(solution)/shard_map/all_to_all | solution.py:48
  50.6 8.6 %copy.223 = bf16[32,128,128]{0,1,2:T(8,128)(2,1)} copy(bf16[32,128,128]{2,1,0:T(8,128)(2,1)} %all-gather.5.cloned.1.call-done) | data formatting | bytes 2097152 | tf_op jit(solution)/shard_map/all_gather | solution.py:34
  59.2 3.6 bitcast_reduce_fusion.1
  64.4 1.8 convert_reduce_fusion
  69.5 22.5 %all-gather.7.cloned.1.call-done = bf16[32,128,128]{2,1,0:T(8,128)(2,1)} async-done(((bf16[32,16,128]{2,1,0:T(8,128)(2,1)}), bf16[32,128,128]{2,1,0:T(8,128)(2,1)}) %all-gather.7.cloned.1.call-update) | async-done | bytes 1048592 | tf_op jit(solution)/shard_map/all_gather | solution.py:34
  92.1 2.9 copy.233
  94.9 4.2 all-to-all-start.1
  99.9 19.8 %all_gather.26 = bf16[128,16,128]{2,1,0:T(8,128)(2,1)} all-gather(bf16[32,16,128]{2,1,0:T(8,128)(2,1)} %get-tuple-element.31), channel_id=1, replica_groups=mesh['row'=4,'col'=8] {'row'}, dimensions={0}, use_global_device_ids=true | all-gather | bytes 655360 | tf_op jit(solution)/shard_map/all_gather | solution.py:42
  119.8 2.5 copy.236
  122.3 2.6 copy.235
  124.9 3.2 copy.237
  128.1 3.0 bitcast_reduce_fusion
  131.7 2.4 copy.238
  134.8 2.7 multiply_reduce_fusion.1
  144.4 2.0 fusion.67
  151.8 9.8 %all_gather.28 = bf16[128,16,128]{2,1,0:T(8,128)(2,1)} all-gather(bf16[32,16,128]{2,1,0:T(8,128)(2,1)S(1)} %add_convert_fusion.1), channel_id=1, replica_groups=mesh['row'=4,'col'=8] {'row'}, dimensions={0}, use_global_device_ids=true | all-gather | bytes 655360 | tf_op jit(solution)/shard_map/all_gather | solution.py:42
  161.6 4.1 all-to-all-start.2
  166.0 8.6 %copy.248 = bf16[32,128,128]{0,1,2:T(8,128)(2,1)} copy(bf16[32,128,128]{2,1,0:T(8,128)(2,1)} %all-gather.7.cloned.1.call-done) | data formatting | bytes 2097152 | tf_op jit(solution)/shard_map/all_gather | solution.py:34
  174.6 8.6 %copy.251 = bf16[32,128,128]{0,1,2:T(8,128)(2,1)} copy(bf16[32,128,128]{2,1,0:T(8,128)(2,1)} %all-gather.9.cloned.1.call-done) | data formatting | bytes 2097152 | tf_op jit(solution)/shard_map/all_gather | solution.py:34
  183.2 2.5 copy.247
  185.7 4.6 %fusion.83 = f32[128,16,32]{2,1,0:T(8,128)} fusion(bf16[128,16,128]{0,1,2:T(8,128)(2,1)} %copy.247, bf16[32,128,128]{0,1,2:T(8,128)(2,1)} %copy.248), kind=kOutput, calls=%fused_computation.151 | convolution fusion | flops 16777216 | bytes 1835008 | tf_op jit(solution)/shard_map/kih,ijh->kjh/dot_general | solution.py:89
  190.3 2.4 copy.249
  192.7 1.9 copy.250
  194.6 2.2 copy.252
  196.8 4.5 %fusion.86 = f32[128,32,16]{1,2,0:T(8,128)} fusion(bf16[16,128,128]{1,0,2:T(8,128)(2,1)} %copy.252, bf16[32,128,128]{0,1,2:T(8,128)(2,1)} %copy.251), kind=kOutput, calls=%fused_computation.154 | convolution fusion | flops 16777216 | bytes 1835008 | tf_op jit(solution)/shard_map/ijh,kjh->kih/dot_general | solution.py:86
  201.3 2.4 copy.253
  203.7 2.4 fusion.18
  206.1 2.0 fusion.16
  210.4 2.0 fusion.55
  216.4 2.2 fusion.22
  218.6 1.6 multiply_reduce_fusion
  224.3 2.0 fusion.68
  230.4 2.0 add_convert_fusion
  234.0 10.2 %all_gather.30 = bf16[128,16,128]{2,1,0:T(8,128)(2,1)S(1)} all-gather(bf16[32,16,128]{2,1,0:T(8,128)(2,1)} %get-tuple-element.32), channel_id=1, replica_groups=mesh['row'=4,'col'=8] {'row'}, dimensions={0}, use_global_device_ids=true | all-gather | bytes 655360 | tf_op jit(solution)/shard_map/all_gather | solution.py:42
  244.1 1.5 copy.265
  245.6 11.2 %all-gather.11.cloned.1.call-done = bf16[32,128,128]{2,1,0:T(8,128)(2,1)} async-done(((bf16[32,16,128]{2,1,0:T(8,128)(2,1)}), bf16[32,128,128]{2,1,0:T(8,128)(2,1)}) %all-gather.11.cloned.1.call-update) | async-done | bytes 1048592 | tf_op jit(solution)/shard_map/all_gather | solution.py:34
  256.8 2.9 copy.262
  259.7 4.4 %all-to-all-start.3 = ((bf16[32,128,128]{2,0,1:T(8,128)(2,1)}), bf16[32,128,128]{2,0,1:T(8,128)(2,1)}, u32[]{:S(2)}, u32[]{:S(2)}) async-start(bf16[32,128,128]{2,0,1:T(8,128)(2,1)} %copy.262), calls=%async_computation.3 | async-start | bytes 2097152 | tf_op jit(solution)/shard_map/all_to_all | solution.py:52
  264.4 2.1 convolution_bitcast_fusion.2
  269.3 6.8 %copy.269 = bf16[32,128,128]{0,1,2:T(8,128)(2,1)} copy(bf16[32,128,128]{2,1,0:T(8,128)(2,1)S(1)} %copy-done.1) | data formatting | bytes 2097152 | tf_op jit(solution)/shard_map/all_gather | solution.py:34
  276.1 3.4 fusion.85
  280.0 1.6 copy.264
  281.7 2.3 copy.266
  284.0 1.9 fusion.84
  291.5 129.8 %all-reduce.13.cloned.1.call-done = (f32[128,640]{1,0:T(8,128)}, f32[128,128]{1,0:T(8,128)}, f32[128,640]{1,0:T(8,128)}, f32[128,128]{1,0:T(8,128)}) async-done(((f32[128,640]{1,0:T(8,128)}, f32[128,128]{1,0:T(8,128)}, f32[128,640]{1,0:T(8,128)}, f32[128,128]{1,0:T(8,128)}), (f32[128,640]{1,0:T(8,128)}, f32[128,128]{1,0:T(8,128)}, f32[128,640]{1,0:T(8,128)}, ...) | async-done | bytes 786448 | tf_op jit(solution)/shard_map/psum | solution.py:157
  421.3 1.5 broadcast_multiply_fusion.2
  422.9 1.9 broadcast_multiply_fusion
  (157 shorter events, 52.7 us)
Async XLA Ops:
  7.2 60.2 %copy-start = (bf16[128,640]{1,0:T(8,128)(2,1)S(1)}, bf16[128,640]{1,0:T(8,128)(2,1)}, u32[]{:S(2)}) copy-start(bf16[128,640]{1,0:T(8,128)(2,1)} %param.12) | copy-start | bytes 491524
  7.2 43.4 %all-gather.5.cloned.1.call-start = ((), (), s32[]{:S(2)}) async-start(), calls=%async_computation.4 | async-start | bytes 1179648 | tf_op jit(solution)/shard_map/all_gather | solution.py:34
  11.2 0.6 copy-start.20
  14.1 78.0 %all-gather.7.cloned.1.call-start = ((), (), s32[]{:S(2)}) async-start(), calls=%async_computation.5 | async-start | bytes 1179648 | tf_op jit(solution)/shard_map/all_gather | solution.py:34
  62.8 1.6 copy-start.5
  63.3 4.0 copy-start.2
  63.7 0.6 copy-start.22
  64.4 1.9 copy-start.17
  66.2 1.1 copy-start.7
  66.6 0.6 copy-start.23
  94.9 27.3 %all-to-all-start.1 = ((bf16[32,128,128]{2,0,1:T(8,128)(2,1)}), bf16[32,128,128]{2,0,1:T(8,128)(2,1)}, u32[]{:S(2)}, u32[]{:S(2)}) async-start(bf16[32,128,128]{2,0,1:T(8,128)(2,1)} %copy.233), calls=%async_computation.1 | async-start | bytes 2097152 | tf_op jit(solution)/shard_map/all_to_all | solution.py:52
  99.2 75.4 %all-gather.9.cloned.1.call-start = ((), (), s32[]{:S(2)}) async-start(), calls=%async_computation.6 | async-start | bytes 1179648 | tf_op jit(solution)/shard_map/all_gather | solution.py:34
  134.8 68.9 %copy-start.19 = (f32[32,16]{1,0:T(8,128)}, f32[32,16]{1,0:T(8,128)S(1)}, u32[]{:S(2)}) copy-start(f32[32,16]{1,0:T(8,128)S(1)} %copy.240) | copy-start | bytes 6148
  161.6 31.0 %all-to-all-start.2 = ((bf16[128,16,128]{2,1,0:T(8,128)(2,1)}), bf16[128,16,128]{2,1,0:T(8,128)(2,1)}, u32[]{:S(2)}, u32[]{:S(2)}) async-start(bf16[128,16,128]{2,1,0:T(8,128)(2,1)} %all_gather.28), calls=%async_computation.2 | async-start | bytes 1048576 | tf_op jit(solution)/shard_map/all_to_all | solution.py:48
  165.8 91.0 %all-gather.11.cloned.1.call-start = ((), (), s32[]{:S(2)}) async-start(), calls=%async_computation.7 | async-start | bytes 1179648 | tf_op jit(solution)/shard_map/all_gather | solution.py:34
  203.7 2.4 copy-start.8
  206.1 2.1 copy-start.26
  206.1 2.1 copy-start.28
  206.1 2.1 copy-start.30
  206.1 2.1 copy-start.32
  206.1 2.1 copy-start.34
  206.1 2.9 copy-start.24
  216.4 2.2 copy-start.3
  216.4 2.2 copy-start.25
  218.6 1.6 copy-start.12
  218.6 5.7 %copy-start.18 = (f32[32,16]{1,0:T(8,128)S(1)}, f32[32,16]{1,0:T(8,128)}, u32[]{:S(2)}) copy-start(f32[32,16]{1,0:T(8,128)} %copy-done.17) | copy-start | bytes 6148
  259.7 4.7 %copy-start.6 = (f32[128,16,32]{0,1,2:T(8,128)S(1)}, f32[128,16,32]{0,1,2:T(8,128)}, u32[]{:S(2)}) copy-start(f32[128,16,32]{0,1,2:T(8,128)} %copy.238) | copy-start | bytes 786436
  259.7 20.3 %all-to-all-start.3 = ((bf16[32,128,128]{2,0,1:T(8,128)(2,1)}), bf16[32,128,128]{2,0,1:T(8,128)(2,1)}, u32[]{:S(2)}, u32[]{:S(2)}) async-start(bf16[32,128,128]{2,0,1:T(8,128)(2,1)} %copy.262), calls=%async_computation.3 | async-start | bytes 2097152 | tf_op jit(solution)/shard_map/all_to_all | solution.py:52
  264.1 2.4 copy-start.4
  264.1 157.2 %all-reduce.13.cloned.1.call-start = ((), (), s32[]{:S(2)}) async-start(), calls=%async_computation.8 | async-start | bytes 1572864 | tf_op jit(solution)/shard_map/psum | solution.py:157
  264.4 2.1 copy-start.13
  266.5 1.2 copy-start.9
  266.5 1.2 copy-start.27
  266.5 1.2 copy-start.29
  266.5 1.2 copy-start.31
  266.5 1.2 copy-start.33
  266.5 1.3 copy-start.35
  267.8 1.5 copy-start.1
  269.3 6.8 %copy-start.11 = (bf16[128,16,128]{0,1,2:T(8,128)(2,1)S(1)}, bf16[128,16,128]{0,1,2:T(8,128)(2,1)}, u32[]{:S(2)}) copy-start(bf16[128,16,128]{0,1,2:T(8,128)(2,1)} %copy.268) | copy-start | bytes 1572868
  281.6 2.3 copy-start.10
  286.3 1.0 copy-start.15
  287.3 1.5 copy-start.16
  288.8 0.9 copy-start.21
  289.6 0.9 copy-start.14
Sparse Core Ops, SparseCore 0:
  14.2 32.2 all-gather.4
  69.6 22.3 all-gather.6
  101.6 24.2 all-gather.8
  232.6 24.2 all-gather.10
  290.4 130.9 all-reduce.12
where the time goes:
time: 434 us; the launch traced here: 431 us
  waiting for transfers between devices  164 us (38%)
  local copies, waits for them, and re-layouts  92.8 us (21%)
  blocking collectives  75.1 us (17%)
  matrix products  41.1 us (9%)
  other arithmetic  30.4 us (7%)
  between operations  14.2 us (3%)
  starting transfers between devices  13.4 us (3%)
    psum x1, waiting for transfers between devices, local(): lax.psum((out_in_part, out_out_part, in_in_part, in_out_part), ('row', 'c...  130 us
    all_gather x4, blocking collectives, rows_of(): lax.all_gather(shortened(tiles), 'row', axis=0, tiled=True)  51.3 us
    all_gather x6, local copies, waits for them, and re-layouts, cols_of(): lax.all_gather(shortened(tiles), 'col', axis=1, tiled=True)  38.3 us
    all_gather x4, waiting for transfers between devices, cols_of(): lax.all_gather(shortened(tiles), 'col', axis=1, tiled=True)  33.8 us
    all_to_all x1, blocking collectives, to_row_blocks(): return lax.all_to_all(panel, 'col', split_axis=0, concat_axis=1, tiled=True)  23.7 us
    unnamed x78, local copies, waits for them, and re-layouts  9.87 us
    all_to_all x4, local copies, waits for them, and re-layouts, to_col_blocks(): return lax.all_to_all(panel, 'row', split_axis=1, concat_axis=0, tiled=True)  9.75 us
  transfers between devices with their start and end apart: 8, of which 3 were waited for; matrix products, arithmetic and copies ran while one was open for 18% of the time, Pallas kernels for 0%

commit v1 on v0

--- a/solution.py
+++ b/solution.py
@@ -45,7 +45,10 @@
 
 
 def to_row_blocks(panel):
-    return lax.all_to_all(panel, "col", split_axis=0, concat_axis=1, tiled=True)
+    report_vector = lambda v0, d0, axis_k: jnp.concatenate(
+        lax.all_to_all(jnp.stack(jnp.split(v0, lax.axis_size("col"), d0), 0), "col", 0, 0), axis_k
+    )
+    return report_vector(panel, 0, 1)
 
 
 def to_col_blocks(panel):

time: 434 us -> 403 us (0.929)
  local copies, waits for them, and re-layouts: 92.8 us -> 78.4 us
  other arithmetic: 30.4 us -> 18.4 us
    unnamed x78 -> x100, local copies, waits for them, and re-layouts: 9.87 us -> 9.82 us
where the time goes in v1:
time: 403 us; the launch traced here: 401 us
  waiting for transfers between devices  164 us (41%)
  local copies, waits for them, and re-layouts  78.4 us (19%)
  blocking collectives  74.7 us (19%)
  matrix products  37.7 us (9%)
  other arithmetic  18.4 us (5%)
  between operations  14.3 us (4%)
  starting transfers between devices  13.4 us (3%)
    psum x1, waiting for transfers between devices, local(): lax.psum((out_in_part, out_out_part, in_in_part, in_out_part), ('row', 'c...  130 us
    all_gather x4, blocking collectives, rows_of(): lax.all_gather(shortened(tiles), 'row', axis=0, tiled=True)  51.2 us
    all_gather x6, local copies, waits for them, and re-layouts, cols_of(): lax.all_gather(shortened(tiles), 'col', axis=1, tiled=True)  38.3 us
    all_gather x4, waiting for transfers between devices, cols_of(): lax.all_gather(shortened(tiles), 'col', axis=1, tiled=True)  33.8 us
    all_to_all x1, blocking collectives, to_row_blocks(): lax.all_to_all(jnp.stack(jnp.split(v0, lax.axis_size('col'), d0), 0), 'co...  23.6 us
    unnamed x100, local copies, waits for them, and re-layouts  9.82 us
    all_to_all x4, local copies, waits for them, and re-layouts, to_col_blocks(): return lax.all_to_all(panel, 'row', split_axis=1, concat_axis=0, tiled=True)  9.75 us
    all_to_all x2, starting transfers between devices, to_col_blocks(): return lax.all_to_all(panel, 'row', split_axis=1, concat_axis=0, tiled=True)  8.62 us
  transfers between devices with their start and end apart: 8, of which 3 were waited for; matrix products, arithmetic and copies ran while one was open for 18% of the time, Pallas kernels for 0%

profile of v1, /device:TPU:0, one launch (start us, length us, event | category | flops | bytes accessed | tf_op | source)
XLA Modules:
  0.0 401.3 jit_solution(14780847981704059782)
XLA Ops:
  11.8 1.4 fusion.53
  14.1 11.5 %all_gather.24 = bf16[128,16,128]{2,1,0:T(8,128)(2,1)S(1)} all-gather(bf16[32,16,128]{2,1,0:T(8,128)(2,1)S(1)} %get-tuple-element.33), channel_id=1, replica_groups=mesh['row'=4,'col'=8] {'row'}, dimensions={0}, use_global_device_ids=true | all-gather | bytes 655360 | tf_op jit(solution)/shard_map/all_gather | solution.py:42
  25.8 23.6 %all_to_all.46 = bf16[8,16,16,128]{3,2,1,0:T(8,128)(2,1)S(1)} all-to-all(bf16[8,16,16,128]{3,2,1,0:T(8,128)(2,1)S(1)} %fusion.69), channel_id=1, replica_groups=mesh['row'=4,'col'=8] {'col'}, dimensions={0} | all-to-all | bytes 1048576 | tf_op jit(solution)/shard_map/all_to_all | solution.py:49
  49.4 1.2 copy.214
  50.6 8.6 %copy.215 = bf16[32,128,128]{0,1,2:T(8,128)(2,1)} copy(bf16[32,128,128]{2,1,0:T(8,128)(2,1)} %all-gather.5.cloned.1.call-done) | data formatting | bytes 2097152 | tf_op jit(solution)/shard_map/all_gather | solution.py:34
  59.2 3.6 bitcast_reduce_fusion.1
  64.4 1.8 convert_reduce_fusion
  67.3 1.3 fusion.50
  69.8 22.6 %all-gather.7.cloned.1.call-done = bf16[32,128,128]{2,1,0:T(8,128)(2,1)} async-done(((bf16[32,16,128]{2,1,0:T(8,128)(2,1)}), bf16[32,128,128]{2,1,0:T(8,128)(2,1)}) %all-gather.7.cloned.1.call-update) | async-done | bytes 1048592 | tf_op jit(solution)/shard_map/all_gather | solution.py:34
  92.4 2.9 copy.225
  95.3 4.2 %all-to-all-start.1 = ((bf16[32,128,128]{2,0,1:T(8,128)(2,1)}), bf16[32,128,128]{2,0,1:T(8,128)(2,1)}, u32[]{:S(2)}, u32[]{:S(2)}) async-start(bf16[32,128,128]{2,0,1:T(8,128)(2,1)} %copy.225), calls=%async_computation.1 | async-start | bytes 2097152 | tf_op jit(solution)/shard_map/all_to_all | solution.py:55
  100.3 19.8 %all_gather.26 = bf16[128,16,128]{2,1,0:T(8,128)(2,1)} all-gather(bf16[32,16,128]{2,1,0:T(8,128)(2,1)} %get-tuple-element.31), channel_id=1, replica_groups=mesh['row'=4,'col'=8] {'row'}, dimensions={0}, use_global_device_ids=true | all-gather | bytes 655360 | tf_op jit(solution)/shard_map/all_gather | solution.py:42
  120.1 2.5 copy.228
  122.6 2.6 copy.227
  125.2 3.2 copy.229
  128.4 3.1 bitcast_reduce_fusion
  131.5 2.4 copy.230
  135.2 2.7 multiply_reduce_fusion.1
  139.6 1.4 fusion.83
  141.2 1.4 add_convert_fusion.1
  142.6 9.1 %all_gather.28 = bf16[128,16,128]{2,1,0:T(8,128)(2,1)S(1)} all-gather(bf16[32,16,128]{2,1,0:T(8,128)(2,1)S(1)} %add_convert_fusion.1), channel_id=1, replica_groups=mesh['row'=4,'col'=8] {'row'}, dimensions={0}, use_global_device_ids=true | all-gather | bytes 655360 | tf_op jit(solution)/shard_map/all_gather | solution.py:42
  156.6 4.1 %all-to-all-start.2 = ((bf16[8,16,16,128]{3,2,1,0:T(8,128)(2,1)}), bf16[8,16,16,128]{3,2,1,0:T(8,128)(2,1)}, u32[]{:S(2)}, u32[]{:S(2)}) async-start(bf16[8,16,16,128]{3,2,1,0:T(8,128)(2,1)} %fusion.61), calls=%async_computation.2 | async-start | bytes 1048576 | tf_op jit(solution)/shard_map/all_to_all | solution.py:49
  161.0 8.6 %copy.240 = bf16[32,128,128]{0,1,2:T(8,128)(2,1)} copy(bf16[32,128,128]{2,1,0:T(8,128)(2,1)} %all-gather.7.cloned.1.call-done) | data formatting | bytes 2097152 | tf_op jit(solution)/shard_map/all_gather | solution.py:34
  169.6 8.6 %copy.243 = bf16[32,128,128]{0,1,2:T(8,128)(2,1)} copy(bf16[32,128,128]{2,1,0:T(8,128)(2,1)} %all-gather.9.cloned.1.call-done) | data formatting | bytes 2097152 | tf_op jit(solution)/shard_map/all_gather | solution.py:34
  178.2 1.5 copy.239
  179.7 3.5 fusion.99
  185.6 1.2 copy.244
  186.8 3.5 fusion.102
  191.5 2.7 fusion.18
  197.1 2.0 fusion.22
  199.0 1.2 multiply_reduce_fusion
  202.0 1.6 copy.260
  203.5 10.7 %all_gather.30 = bf16[128,16,128]{2,1,0:T(8,128)(2,1)S(1)} all-gather(bf16[32,16,128]{2,1,0:T(8,128)(2,1)S(1)} %copy-done.11), channel_id=1, replica_groups=mesh['row'=4,'col'=8] {'row'}, dimensions={0}, use_global_device_ids=true | all-gather | bytes 655360 | tf_op jit(solution)/shard_map/all_gather | solution.py:42
  214.2 1.5 copy.257
  215.7 11.2 %all-gather.11.cloned.1.call-done = bf16[32,128,128]{2,1,0:T(8,128)(2,1)} async-done(((bf16[32,16,128]{2,1,0:T(8,128)(2,1)}), bf16[32,128,128]{2,1,0:T(8,128)(2,1)}) %all-gather.11.cloned.1.call-update) | async-done | bytes 1048592 | tf_op jit(solution)/shard_map/all_gather | solution.py:34
  226.8 2.9 copy.254
  229.7 4.4 %all-to-all-start.3 = ((bf16[32,128,128]{2,0,1:T(8,128)(2,1)}), bf16[32,128,128]{2,0,1:T(8,128)(2,1)}, u32[]{:S(2)}, u32[]{:S(2)}) async-start(bf16[32,128,128]{2,0,1:T(8,128)(2,1)} %copy.254), calls=%async_computation.3 | async-start | bytes 2097152 | tf_op jit(solution)/shard_map/all_to_all | solution.py:55
  234.4 2.1 convolution_bitcast_fusion.2
  237.8 1.5 convolution_bitcast_fusion
  239.2 6.8 %copy.261 = bf16[32,128,128]{0,1,2:T(8,128)(2,1)} copy(bf16[32,128,128]{2,1,0:T(8,128)(2,1)S(1)} %copy-done.2) | data formatting | bytes 2097152 | tf_op jit(solution)/shard_map/all_gather | solution.py:34
  246.0 3.4 fusion.101
  249.9 1.6 copy.256
  251.5 2.3 copy.258
  253.8 1.9 fusion.100
  257.2 1.5 convolution_bitcast_fusion.1
  261.4 129.9 %all-reduce.13.cloned.1.call-done = (f32[128,640]{1,0:T(8,128)}, f32[128,128]{1,0:T(8,128)}, f32[128,640]{1,0:T(8,128)}, f32[128,128]{1,0:T(8,128)}) async-done(((f32[128,640]{1,0:T(8,128)}, f32[128,128]{1,0:T(8,128)}, f32[128,640]{1,0:T(8,128)}, f32[128,128]{1,0:T(8,128)}), (f32[128,640]{1,0:T(8,128)}, f32[128,128]{1,0:T(8,128)}, f32[128,640]{1,0:T(8,128)}, ...) | async-done | bytes 786448 | tf_op jit(solution)/shard_map/psum | solution.py:160
  391.3 1.5 broadcast_multiply_fusion.2
  392.8 1.9 broadcast_multiply_fusion
  (181 shorter events, 32.8 us)
Async XLA Ops:
  7.2 60.2 %copy-start = (bf16[128,640]{1,0:T(8,128)(2,1)S(1)}, bf16[128,640]{1,0:T(8,128)(2,1)}, u32[]{:S(2)}) copy-start(bf16[128,640]{1,0:T(8,128)(2,1)} %param.12) | copy-start | bytes 491524
  7.2 43.4 %all-gather.5.cloned.1.call-start = ((), (), s32[]{:S(2)}) async-start(), calls=%async_computation.4 | async-start | bytes 1179648 | tf_op jit(solution)/shard_map/all_gather | solution.py:34
  11.2 0.6 copy-start.24
  14.1 78.3 %all-gather.7.cloned.1.call-start = ((), (), s32[]{:S(2)}) async-start(), calls=%async_computation.5 | async-start | bytes 1179648 | tf_op jit(solution)/shard_map/all_gather | solution.py:34
  62.8 1.6 copy-start.5
  63.3 4.0 copy-start.3
  63.7 0.6 copy-start.26
  64.4 1.9 copy-start.17
  66.2 1.1 copy-start.7
  66.6 0.6 copy-start.28
  68.6 66.6 %copy-start.1 = (f32[32,16,640]{2,1,0:T(8,128)}, f32[32,16,640]{2,1,0:T(8,128)S(1)}, u32[]{:S(2)}) copy-start(f32[32,16,640]{2,1,0:T(8,128)S(1)} %fusion.50) | copy-start | bytes 3932164
  95.3 27.3 %all-to-all-start.1 = ((bf16[32,128,128]{2,0,1:T(8,128)(2,1)}), bf16[32,128,128]{2,0,1:T(8,128)(2,1)}, u32[]{:S(2)}, u32[]{:S(2)}) async-start(bf16[32,128,128]{2,0,1:T(8,128)(2,1)} %copy.225), calls=%async_computation.1 | async-start | bytes 2097152 | tf_op jit(solution)/shard_map/all_to_all | solution.py:55
  99.5 70.1 %all-gather.9.cloned.1.call-start = ((), (), s32[]{:S(2)}) async-start(), calls=%async_computation.6 | async-start | bytes 1179648 | tf_op jit(solution)/shard_map/all_gather | solution.py:34
  135.2 56.3 %copy-start.19 = (f32[32,16]{1,0:T(8,128)}, f32[32,16]{1,0:T(8,128)S(1)}, u32[]{:S(2)}) copy-start(f32[32,16]{1,0:T(8,128)S(1)} %copy.232) | copy-start | bytes 6148
  139.6 1.6 copy-start.21
  156.6 27.8 %all-to-all-start.2 = ((bf16[8,16,16,128]{3,2,1,0:T(8,128)(2,1)}), bf16[8,16,16,128]{3,2,1,0:T(8,128)(2,1)}, u32[]{:S(2)}, u32[]{:S(2)}) async-start(bf16[8,16,16,128]{3,2,1,0:T(8,128)(2,1)} %fusion.61), calls=%async_computation.2 | async-start | bytes 1048576 | tf_op jit(solution)/shard_map/all_to_all | solution.py:49
  160.8 66.1 %all-gather.11.cloned.1.call-start = ((), (), s32[]{:S(2)}) async-start(), calls=%async_computation.7 | async-start | bytes 1179648 | tf_op jit(solution)/shard_map/all_gather | solution.py:34
  190.3 1.2 copy-start.6
  191.5 3.4 copy-start.8
  194.2 0.7 copy-start.30
  194.2 1.5 copy-start.32
  194.2 1.5 copy-start.34
  194.2 1.5 copy-start.36
  194.2 1.5 copy-start.38
  194.9 0.9 copy-start.29
  194.9 2.2 copy-start.14
  195.7 3.3 copy-start.4
  199.0 37.5 %copy-start.12 = (bf16[32,16,128]{2,1,0:T(8,128)(2,1)}, bf16[32,16,128]{2,1,0:T(8,128)(2,1)S(1)}, u32[]{:S(2)}) copy-start(bf16[32,16,128]{2,1,0:T(8,128)(2,1)S(1)} %get-tuple-element.13) | copy-start | bytes 393220
  199.0 1.3 copy-start.27
  199.0 1.4 copy-start.18
  200.3 3.2 copy-start.11
  229.7 4.7 %copy-start.20 = (f32[32,16]{1,0:T(8,128)S(1)}, f32[32,16]{1,0:T(8,128)}, u32[]{:S(2)}) copy-start(f32[32,16]{1,0:T(8,128)} %copy-done.19) | copy-start | bytes 6148
  229.7 4.7 %copy-start.22 = (f32[32,16]{1,0:T(8,128)S(1)}, f32[32,16]{1,0:T(8,128)}, u32[]{:S(2)}) copy-start(f32[32,16]{1,0:T(8,128)} %copy-done.21) | copy-start | bytes 6148
  229.7 4.7 %copy-start.23 = (bf16[32,16,128]{2,1,0:T(8,128)(2,1)S(1)}, bf16[32,16,128]{2,1,0:T(8,128)(2,1)}, u32[]{:S(2)}) copy-start(bf16[32,16,128]{2,1,0:T(8,128)(2,1)} %param.8) | copy-start | bytes 393220
  229.7 20.2 %all-to-all-start.3 = ((bf16[32,128,128]{2,0,1:T(8,128)(2,1)}), bf16[32,128,128]{2,0,1:T(8,128)(2,1)}, u32[]{:S(2)}, u32[]{:S(2)}) async-start(bf16[32,128,128]{2,0,1:T(8,128)(2,1)} %copy.254), calls=%async_computation.3 | async-start | bytes 2097152 | tf_op jit(solution)/shard_map/all_to_all | solution.py:55
  234.1 157.2 %all-reduce.13.cloned.1.call-start = ((), (), s32[]{:S(2)}) async-start(), calls=%async_computation.8 | async-start | bytes 1572864 | tf_op jit(solution)/shard_map/psum | solution.py:160
  236.5 1.1 copy-start.31
  236.5 1.1 copy-start.33
  236.5 1.1 copy-start.35
  236.5 1.2 copy-start.37
  236.5 1.2 copy-start.39
  237.7 1.5 copy-start.2
  239.2 6.8 %copy-start.10 = (bf16[128,16,128]{0,1,2:T(8,128)(2,1)S(1)}, bf16[128,16,128]{0,1,2:T(8,128)(2,1)}, u32[]{:S(2)}) copy-start(bf16[128,16,128]{0,1,2:T(8,128)(2,1)} %copy.260) | copy-start | bytes 1572868
  251.5 2.3 copy-start.9
  256.2 1.0 copy-start.15
  257.2 1.5 copy-start.16
  258.7 0.9 copy-start.25
  259.5 0.9 copy-start.13
Sparse Core Ops, SparseCore 0:
  14.2 32.2 all-gather.4
  69.9 22.4 all-gather.6
  101.9 24.2 all-gather.8
  202.1 24.7 all-gather.10
  260.2 130.9 all-reduce.12
